TPU v7x, 32 devices: a whole 2x2x4 slice. The times are simulated.
32 devices in a mesh: tm: 4 (over y, x), chan: 8 (over z, core).
Axes of the slice: x: 2, y: 2, z: 4, core: 2. Of those that a mesh axis runs over, the one named last changes fastest.
Arguments:
- observations: float32 [16, 64, 16384], P('chan', None, 'tm'), may hold values from -6 to 6
- transition: float32 [16, 128, 128], P('chan'), may hold values from -1 to 1, as said below
- obs_map: float32 [16, 64, 128], P('chan'), may hold values from -0.25 to 0.25
- measured_weighting: float32 [16, 64], P('chan'), may hold values from 0.05 to 0.5
- obs_precision: float32 [16, 64], P('chan'), may hold values from 0.3 to 9
- fading: float32 [16, 16384], P('chan', 'tm'), may hold values from 0.5 to 1
Outputs:
- states: float32 [16, 128, 16384], P('chan', None, 'tm')
- batch_nis: float32 [128], P('tm')
Inputs may be any that keep to these rules, and one draw needn't show every extreme that they name: Each channel's transition is symmetric with all eigenvalues of magnitude below one.
All inputs are finite; a program needn't handle non-finite values.
Results may differ from a plain program's by a relative error of at most 0.0003.
Values sent between devices are 32-bit elements; how exact they have to be, the bound alone decides.
A program may use at most 64 MiB of HBM per device.

v0:
```python
import functools

import jax
import jax.numpy as jnp
from jax import lax
from jax.experimental import pallas as pl
from jax.experimental.pallas import tpu as pltpu
from jax.sharding import PartitionSpec as P

MB_FRAMES = 128
CHUNK = 16
HIGHEST = lax.Precision.HIGHEST
F32 = jnp.float32
BF16 = jnp.bfloat16


def dot(a, b, dims=((1,), (0,)), precision=HIGHEST):
    return lax.dot_general(a, b, (dims, ((), ())), precision=precision, preferred_element_type=F32)


def halves(x):
    high = x.astype(BF16)
    low = (x - high.astype(F32)).astype(BF16)
    return high, low


def rows_split(x):
    return jnp.concatenate(halves(x), axis=1)


def pack(weight):
    high, low = halves(weight)
    top = jnp.concatenate([high, low], axis=1)
    return jnp.concatenate([top, top], axis=0)


def fast(split, packed):
    both = dot(split, packed, precision=None)
    half = both.shape[1] // 2
    return both[:, :half] + both[:, half:]


def shifted(x, reach, fill, row):
    return jnp.where(row >= reach, pltpu.roll(x, reach, 0), fill)


def kernel(
    tm, chan, y_hbm, trans_ref, map_ref, weight_ref, prec_ref, fade_ref, states_hbm, nis_ref,
    y_ref, yt_ref, ft_ref, xt_ref, out_ref, end_src, end_got, nis_src, nis_got,
    in_sem, out_sem, end_send, end_recv, nis_send, nis_recv,
):
    channels, obs, frames = y_ref.shape
    state = trans_ref.shape[1]
    length = CHUNK
    count = frames // length
    my_tm, my_chan = lax.axis_index("tm"), lax.axis_index("chan")

    def peer(axis, size, mine, offset):
        return {axis: lax.rem(mine + offset, size)}

    peers = [peer("tm", tm, my_tm, d) for d in range(1, tm)]
    peers += [peer("chan", chan, my_chan, d) for d in range(1, chan)]
    barrier = pltpu.get_barrier_semaphore()
    for target in peers:
        pl.semaphore_signal(barrier, inc=1, device_id=target, device_id_type=pl.DeviceIdType.MESH)
    load = pltpu.make_async_copy(y_hbm, y_ref, in_sem)
    load.start()

    each = range(channels)
    lanes = channels * obs
    eye = lax.broadcasted_iota(jnp.int32, (obs, obs), 0) == lax.broadcasted_iota(jnp.int32, (obs, obs), 1)
    owner = lax.broadcasted_iota(jnp.int32, (1, lanes), 1) // obs

    fade = fade_ref[...]
    ft_ref[...] = jnp.transpose(jnp.concatenate([fade] * (8 // channels), axis=0))

    def fade_at(step):
        return ft_ref[pl.ds(step, count, stride=length), :]

    def fade_lanes(columns):
        out = jnp.broadcast_to(columns[:, 0:1], (count, lanes))
        for c in each[1:]:
            out = jnp.where(owner == c, columns[:, c : c + 1], out)
        return out

    weighted, closed, map_trans = [], [], []
    for c in each:
        column = jnp.sum(jnp.where(eye, weight_ref[c : c + 1, :], 0.0), axis=1, keepdims=True)
        observe = map_ref[c]
        weighted.append(observe * column)
        moved = dot(observe, trans_ref[c])
        map_trans.append(jnp.transpose(moved))
        closed.append(jnp.transpose(trans_ref[c]) - dot(moved, weighted[c], ((0,), (0,))))

    stacks, power = list(weighted), list(closed)
    reach = 1
    while reach < length:
        for c in each:
            stacks[c] = jnp.concatenate([stacks[c], dot(stacks[c], power[c])], axis=0)
            power[c] = dot(power[c], power[c])
        reach *= 2

    def spread(blocks):
        rows = []
        for c in each:
            parts = [blocks[c] if d == c else jnp.zeros_like(blocks[c]) for d in each]
            rows.append(jnp.concatenate(parts, axis=1))
        return jnp.concatenate(rows, axis=0)

    def inject_weight(blocks):
        high, low = halves(spread(blocks))
        return jnp.concatenate([high, high, low], axis=0)

    def inject(values, weight):
        high, low = halves(values)
        return dot(jnp.concatenate([high, low, high], axis=1), weight, precision=None)

    load.wait()
    block = min(frames, 512)
    for start in range(0, frames, block):
        piece = y_ref[:, :, start : start + block].reshape(lanes, block)
        yt_ref[start : start + block, :] = jnp.transpose(piece)

    def obs_at(step):
        return yt_ref[pl.ds(step, count, stride=length), :]

    ends = jnp.zeros((count, channels * state), F32)
    decay = jnp.ones((count, lanes), F32)
    for step in reversed(range(length)):
        age = length - 1 - step
        blocks = [stacks[c][age * obs : (age + 1) * obs] for c in each]
        ends = ends + inject(obs_at(step) * decay, inject_weight(blocks))
        decay = decay * fade_lanes(fade_at(step))

    row = lax.broadcasted_iota(jnp.int32, (count, state), 0)
    sums = [ends[:, c * state : (c + 1) * state] for c in each]
    factors = [jnp.broadcast_to(decay[:, c * obs : c * obs + 1], (count, state)) for c in each]
    packed = []
    reach = 1
    while reach < count:
        packed.append([pack(power[c]) for c in each])
        for c in each:
            before = rows_split(shifted(sums[c], reach, 0.0, row))
            sums[c] = sums[c] + factors[c] * fast(before, packed[-1][c])
            factors[c] = factors[c] * shifted(factors[c], reach, 1.0, row)
            power[c] = dot(power[c], power[c])
        reach *= 2

    last = [part[c][count - 1 : count, :] for part in (sums, factors) for c in each]
    end_src[...] = jnp.concatenate(last + [jnp.zeros((8 - len(last), state), F32)], axis=0)
    pl.semaphore_wait(barrier, len(peers))
    sends = []
    for d in range(1, tm):
        copy = pltpu.make_async_remote_copy(
            src_ref=end_src, dst_ref=end_got.at[d - 1], send_sem=end_send.at[d - 1],
            recv_sem=end_recv.at[d - 1], device_id=peers[d - 1], device_id_type=pl.DeviceIdType.MESH,
        )
        copy.start()
        sends.append(copy)

    sums = [shifted(sums[c], 1, 0.0, row) for c in each]
    factors = [shifted(factors[c], 1, 1.0, row) for c in each]
    step_weight = [pack(closed[c]) for c in each]
    pred_weight = []
    for c in each:
        parts = [map_trans[c] if d == c else jnp.zeros_like(map_trans[c]) for d in each]
        pred_weight.append(pack(jnp.concatenate(parts, axis=1)))
    now_weight = inject_weight(weighted)
    section = [pack(power[c]) for c in each]

    for copy in sends:
        copy.wait()

    enter = [jnp.zeros((8, state), F32) for c in each]
    for j in range(tm - 1):
        slot = jnp.maximum(lax.rem(my_tm - j + tm, tm) - 1, 0)
        got = end_got[slot]
        for c in each:
            value = jnp.broadcast_to(got[c : c + 1, :], (8, state))
            if j > 0:
                value = value + got[channels + c : channels + c + 1, :] * fast(
                    rows_split(enter[c]), section[c]
                )
            enter[c] = jnp.where(j < my_tm, value, enter[c])

    x = []
    small = lax.broadcasted_iota(jnp.int32, (8, state), 0)
    for c in each:
        carried = enter[c]
        for level, weights in enumerate(packed):
            further = fast(rows_split(carried), weights[c])
            size = 1 << level
            if size < 8:
                carried = jnp.where(small < size, carried, pltpu.roll(further, size, 0))
            else:
                carried = jnp.concatenate([carried, further], axis=0)
        x.append(sums[c] + factors[c] * carried[:count])

    prec = jnp.concatenate([prec_ref[c : c + 1, :] for c in each], axis=1)
    norms = jnp.zeros((count, lanes), F32)
    for step in range(length):
        observed = obs_at(step)
        columns = fade_at(step)
        added = inject(observed, now_weight)
        innovation = observed
        for c in each:
            split = rows_split(x[c])
            wide = jnp.broadcast_to(columns[:, c : c + 1], (count, state))
            innovation = innovation - columns[:, c : c + 1] * fast(split, pred_weight[c])
            x[c] = wide * fast(split, step_weight[c]) + added[:, c * state : (c + 1) * state]
            xt_ref[c, pl.ds(step, count, stride=length), :] = x[c]
        norms = norms + prec * innovation * innovation

    batches = nis_ref.shape[1]
    per_batch = jnp.sum(norms.reshape(batches, count // batches, lanes), axis=1)
    nis_src[...] = dot(jnp.ones((8, lanes), F32), per_batch, ((1,), (1,)))
    sends = []
    for d in range(1, chan):
        copy = pltpu.make_async_remote_copy(
            src_ref=nis_src, dst_ref=nis_got.at[d - 1], send_sem=nis_send.at[d - 1],
            recv_sem=nis_recv.at[d - 1], device_id=peers[tm - 1 + d - 1],
            device_id_type=pl.DeviceIdType.MESH,
        )
        copy.start()
        sends.append(copy)

    stores = []
    for c in each:
        for index, start in enumerate(range(0, frames, block)):
            out_ref[c, :, start : start + block] = jnp.transpose(xt_ref[c, start : start + block, :])
            store = pltpu.make_async_copy(
                out_ref.at[c, :, pl.ds(start, block)],
                states_hbm.at[c, :, pl.ds(start, block)],
                out_sem.at[c, index],
            )
            store.start()
            stores.append(store)

    for copy in sends:
        copy.wait()
    total = nis_src[0:1, :]
    for d in range(1, chan):
        total = total + nis_got[d - 1, 0:1, :]
    nis_ref[...] = total / (channels * chan * MB_FRAMES * obs)
    for store in stores:
        store.wait()


def per_device(tm, chan, observations, transition, obs_map, measured_weighting, obs_precision, fading):
    channels, obs, frames = observations.shape
    state = transition.shape[1]
    batches = frames // MB_FRAMES
    lanes = channels * obs
    vmem = pl.BlockSpec(memory_space=pltpu.VMEM)
    hbm = pl.BlockSpec(memory_space=pl.ANY)
    dma = pltpu.SemaphoreType.DMA
    blocks = frames // min(frames, 512)
    states, nis = pl.pallas_call(
        functools.partial(kernel, tm, chan),
        out_shape=(
            jax.ShapeDtypeStruct((channels, state, frames), F32),
            jax.ShapeDtypeStruct((1, batches), F32),
        ),
        in_specs=[hbm] + [vmem] * 5,
        out_specs=(hbm, vmem),
        scratch_shapes=[
            pltpu.VMEM((channels, obs, frames), F32),
            pltpu.VMEM((frames, lanes), F32),
            pltpu.VMEM((frames, 8), F32),
            pltpu.VMEM((channels, frames, state), F32),
            pltpu.VMEM((channels, state, frames), F32),
            pltpu.VMEM((8, state), F32),
            pltpu.VMEM((max(tm - 1, 1), 8, state), F32),
            pltpu.VMEM((8, batches), F32),
            pltpu.VMEM((max(chan - 1, 1), 8, batches), F32),
            dma(()),
            dma((channels, blocks)),
            dma((max(tm - 1, 1),)),
            dma((max(tm - 1, 1),)),
            dma((max(chan - 1, 1),)),
            dma((max(chan - 1, 1),)),
        ],
        compiler_params=pltpu.CompilerParams(
            collective_id=0, has_side_effects=True, vmem_limit_bytes=56 * 1024 * 1024
        ),
        name="filter",
    )(observations, transition, obs_map, measured_weighting, obs_precision, fading)
    return states, nis.reshape(batches)


def solution(mesh):
    in_specs = (
        P("chan", None, "tm"),
        P("chan", None, None),
        P("chan", None, None),
        P("chan", None),
        P("chan", None),
        P("chan", "tm"),
    )
    out_specs = (P("chan", None, "tm"), P("tm"))
    body = functools.partial(per_device, mesh.shape["tm"], mesh.shape["chan"])
    return jax.shard_map(body, mesh=mesh, in_specs=in_specs, out_specs=out_specs, check_vma=False)
```

profile of v0, /device:TPU:0, one launch (start us, length us, event | category | flops | bytes accessed | tf_op | source)
XLA Modules:
  0.0 33.6 jit_solution(5169810465675869850)
XLA Ops:
  0.6 27.7 %filter.1 = (f32[2,128,4096]{2,1,0:T(8,128)}, f32[1,32]{1,0:T(1,128)}) custom-call(f32[2,64,4096]{2,1,0:T(8,128)} %y_hbm.1, f32[2,128,128]{2,1,0:T(8,128)} %trans_ref.1, f32[2,64,128]{2,1,0:T(8,128)} %map_ref.1, f32[2,64]{1,0:T(2,128)} %weight_ref.1, f32[2,64]{1,0:T(2,128)} %prec_ref.1, f32[2,4096]{1,0:T(2,128)} %fade_ref.1), custom_call_target="tpu_custom_call" | custom-call | tf_op jit(solution)/shard_map/filter/pallas_call | solution.py:258
  28.4 0.0 copy-start
  28.4 4.7 %copy.10 = f32[2,128,4096]{2,1,0:T(8,128)} copy(f32[2,128,4096]{2,1,0:T(8,128)} %get-tuple-element.8) | data formatting | bytes 8388608
  33.0 0.0 copy-done
  33.0 0.5 %copy.11 = f32[32]{0:T(128)} copy(f32[32]{0:T(128)S(1)} %bitcast.1) | data formatting | bytes 256
Async XLA Ops:
  28.4 4.7 %copy-start = (f32[1,32]{1,0:T(1,128)S(1)}, f32[1,32]{1,0:T(1,128)}, u32[]{:S(2)}) copy-start(f32[1,32]{1,0:T(1,128)} %get-tuple-element.5) | copy-start | bytes 388
where the time goes:
time: 33.7 us; the launch traced here: 33.6 us
  Pallas kernels  27.7 us (82%)
  local copies, waits for them, and re-layouts  5.17 us (15%)
  between operations  0.65 us (2%)
    pallas_call x1, Pallas kernels, per_device(): pl.pallas_call(functools.partial(kernel, tm, chan), out_shape=(jax.ShapeD...  27.7 us
    unnamed x4, local copies, waits for them, and re-layouts  5.17 us

commit v1 on v0

--- a/solution.py
+++ b/solution.py
@@ -8,7 +8,9 @@
 from jax.sharding import PartitionSpec as P
 
 MB_FRAMES = 128
-CHUNK = 16
+LANES = 128
+GROUP = 8
+CHUNK = LANES // GROUP
 HIGHEST = lax.Precision.HIGHEST
 F32 = jnp.float32
 BF16 = jnp.bfloat16
@@ -40,13 +42,19 @@
     return both[:, :half] + both[:, half:]
 
 
+def regroup(x, groups):
+    place = lax.broadcasted_iota(jnp.int32, x.shape, 1)
+    source = (place % groups) * (LANES // groups) + place // groups
+    return jnp.take_along_axis(x, source, axis=1, mode="promise_in_bounds")
+
+
 def shifted(x, reach, fill, row):
     return jnp.where(row >= reach, pltpu.roll(x, reach, 0), fill)
 
 
 def kernel(
     tm, chan, y_hbm, trans_ref, map_ref, weight_ref, prec_ref, fade_ref, states_hbm, nis_ref,
-    y_ref, yt_ref, ft_ref, xt_ref, out_ref, end_src, end_got, nis_src, nis_got,
+    y_ref, yt_ref, ft_ref, xt_ref, end_src, end_got, nis_src, nis_got,
     in_sem, out_sem, end_send, end_recv, nis_send, nis_recv,
 ):
     channels, obs, frames = y_ref.shape
@@ -71,11 +79,13 @@
     eye = lax.broadcasted_iota(jnp.int32, (obs, obs), 0) == lax.broadcasted_iota(jnp.int32, (obs, obs), 1)
     owner = lax.broadcasted_iota(jnp.int32, (1, lanes), 1) // obs
 
-    fade = fade_ref[...]
-    ft_ref[...] = jnp.transpose(jnp.concatenate([fade] * (8 // channels), axis=0))
+    fade = jnp.concatenate([fade_ref[...]] * (8 // channels), axis=0)
+    for b in range(frames // LANES):
+        piece = regroup(fade[:, b * LANES : (b + 1) * LANES], GROUP)
+        ft_ref[b] = jnp.transpose(piece).reshape(length, GROUP, 8)
 
     def fade_at(step):
-        return ft_ref[pl.ds(step, count, stride=length), :]
+        return ft_ref[:, step].reshape(count, 8)
 
     def fade_lanes(columns):
         out = jnp.broadcast_to(columns[:, 0:1], (count, lanes))
@@ -92,13 +102,22 @@
         map_trans.append(jnp.transpose(moved))
         closed.append(jnp.transpose(trans_ref[c]) - dot(moved, weighted[c], ((0,), (0,))))
 
+    load.wait()
+    blocks_all = frames // LANES
+
+    def turn(first, last):
+        for b in range(first, last):
+            piece = y_ref[:, :, b * LANES : (b + 1) * LANES].reshape(lanes, LANES)
+            yt_ref[b] = jnp.transpose(regroup(piece, GROUP)).reshape(length, GROUP, lanes)
+
     stacks, power = list(weighted), list(closed)
-    reach = 1
-    while reach < length:
-        for c in each:
-            stacks[c] = jnp.concatenate([stacks[c], dot(stacks[c], power[c])], axis=0)
+    rounds = length.bit_length() - 1
+    for level in range(rounds):
+        turn(level * blocks_all // rounds, (level + 1) * blocks_all // rounds)
+        for c in each:
+            older = fast(rows_split(stacks[c]), pack(power[c]))
+            stacks[c] = jnp.concatenate([stacks[c], older], axis=0)
             power[c] = dot(power[c], power[c])
-        reach *= 2
 
     def spread(blocks):
         rows = []
@@ -115,36 +134,42 @@
         high, low = halves(values)
         return dot(jnp.concatenate([high, low, high], axis=1), weight, precision=None)
 
-    load.wait()
-    block = min(frames, 512)
-    for start in range(0, frames, block):
-        piece = y_ref[:, :, start : start + block].reshape(lanes, block)
-        yt_ref[start : start + block, :] = jnp.transpose(piece)
-
     def obs_at(step):
-        return yt_ref[pl.ds(step, count, stride=length), :]
+        return yt_ref[:, step].reshape(count, lanes)
 
     ends = jnp.zeros((count, channels * state), F32)
     decay = jnp.ones((count, lanes), F32)
+    packed = []
+    levels = count.bit_length() - 1
+    every = max(length // levels, 1)
     for step in reversed(range(length)):
         age = length - 1 - step
         blocks = [stacks[c][age * obs : (age + 1) * obs] for c in each]
         ends = ends + inject(obs_at(step) * decay, inject_weight(blocks))
         decay = decay * fade_lanes(fade_at(step))
+        if len(packed) < levels and age % every == 0:
+            packed.append([pack(power[c]) for c in each])
+            power = [dot(power[c], power[c]) for c in each]
 
     row = lax.broadcasted_iota(jnp.int32, (count, state), 0)
     sums = [ends[:, c * state : (c + 1) * state] for c in each]
     factors = [jnp.broadcast_to(decay[:, c * obs : c * obs + 1], (count, state)) for c in each]
-    packed = []
-    reach = 1
-    while reach < count:
+    while len(packed) < levels:
         packed.append([pack(power[c]) for c in each])
-        for c in each:
-            before = rows_split(shifted(sums[c], reach, 0.0, row))
-            sums[c] = sums[c] + factors[c] * fast(before, packed[-1][c])
-            factors[c] = factors[c] * shifted(factors[c], reach, 1.0, row)
-            power[c] = dot(power[c], power[c])
-        reach *= 2
+        power = [dot(power[c], power[c]) for c in each]
+    for level in range(levels):
+        reach = 1 << level
+        for c in each:
+            if reach < GROUP:
+                before = rows_split(shifted(sums[c], reach, 0.0, row))
+                sums[c] = sums[c] + factors[c] * fast(before, packed[level][c])
+                factors[c] = factors[c] * shifted(factors[c], reach, 1.0, row)
+            else:
+                rest = count - reach
+                moved = factors[c][reach:] * fast(rows_split(sums[c][:rest]), packed[level][c])
+                sums[c] = jnp.concatenate([sums[c][:reach], sums[c][reach:] + moved], axis=0)
+                joined = factors[c][reach:] * factors[c][:rest]
+                factors[c] = jnp.concatenate([factors[c][:reach], joined], axis=0)
 
     last = [part[c][count - 1 : count, :] for part in (sums, factors) for c in each]
     end_src[...] = jnp.concatenate(last + [jnp.zeros((8 - len(last), state), F32)], axis=0)
@@ -198,6 +223,7 @@
 
     prec = jnp.concatenate([prec_ref[c : c + 1, :] for c in each], axis=1)
     norms = jnp.zeros((count, lanes), F32)
+    stores = []
     for step in range(length):
         observed = obs_at(step)
         columns = fade_at(step)
@@ -208,7 +234,12 @@
             wide = jnp.broadcast_to(columns[:, c : c + 1], (count, state))
             innovation = innovation - columns[:, c : c + 1] * fast(split, pred_weight[c])
             x[c] = wide * fast(split, step_weight[c]) + added[:, c * state : (c + 1) * state]
-            xt_ref[c, pl.ds(step, count, stride=length), :] = x[c]
+            xt_ref[c, :, step] = x[c].reshape(blocks_all, GROUP, state)
+            store = pltpu.make_async_copy(
+                xt_ref.at[c, :, step], states_hbm.at[c, :, step], out_sem.at[c, step]
+            )
+            store.start()
+            stores.append(store)
         norms = norms + prec * innovation * innovation
 
     batches = nis_ref.shape[1]
@@ -224,18 +255,6 @@
         copy.start()
         sends.append(copy)
 
-    stores = []
-    for c in each:
-        for index, start in enumerate(range(0, frames, block)):
-            out_ref[c, :, start : start + block] = jnp.transpose(xt_ref[c, start : start + block, :])
-            store = pltpu.make_async_copy(
-                out_ref.at[c, :, pl.ds(start, block)],
-                states_hbm.at[c, :, pl.ds(start, block)],
-                out_sem.at[c, index],
-            )
-            store.start()
-            stores.append(store)
-
     for copy in sends:
         copy.wait()
     total = nis_src[0:1, :]
@@ -246,6 +265,12 @@
         store.wait()
 
 
+def turn_states(x_ref, out_ref):
+    for start in range(0, x_ref.shape[1], LANES):
+        piece = jnp.transpose(x_ref[0, start : start + LANES, :])
+        out_ref[0, :, start : start + LANES] = regroup(piece, CHUNK)
+
+
 def per_device(tm, chan, observations, transition, obs_map, measured_weighting, obs_precision, fading):
     channels, obs, frames = observations.shape
     state = transition.shape[1]
@@ -254,27 +279,26 @@
     vmem = pl.BlockSpec(memory_space=pltpu.VMEM)
     hbm = pl.BlockSpec(memory_space=pl.ANY)
     dma = pltpu.SemaphoreType.DMA
-    blocks = frames // min(frames, 512)
-    states, nis = pl.pallas_call(
+    grouped = (channels, frames // LANES, CHUNK, GROUP, state)
+    turned, nis = pl.pallas_call(
         functools.partial(kernel, tm, chan),
         out_shape=(
-            jax.ShapeDtypeStruct((channels, state, frames), F32),
+            jax.ShapeDtypeStruct(grouped, F32),
             jax.ShapeDtypeStruct((1, batches), F32),
         ),
         in_specs=[hbm] + [vmem] * 5,
         out_specs=(hbm, vmem),
         scratch_shapes=[
             pltpu.VMEM((channels, obs, frames), F32),
-            pltpu.VMEM((frames, lanes), F32),
-            pltpu.VMEM((frames, 8), F32),
-            pltpu.VMEM((channels, frames, state), F32),
-            pltpu.VMEM((channels, state, frames), F32),
+            pltpu.VMEM((frames // LANES, CHUNK, GROUP, lanes), F32),
+            pltpu.VMEM((frames // LANES, CHUNK, GROUP, 8), F32),
+            pltpu.VMEM(grouped, F32),
             pltpu.VMEM((8, state), F32),
             pltpu.VMEM((max(tm - 1, 1), 8, state), F32),
             pltpu.VMEM((8, batches), F32),
             pltpu.VMEM((max(chan - 1, 1), 8, batches), F32),
             dma(()),
-            dma((channels, blocks)),
+            dma((channels, CHUNK)),
             dma((max(tm - 1, 1),)),
             dma((max(tm - 1, 1),)),
             dma((max(chan - 1, 1),)),
@@ -285,6 +309,15 @@
         ),
         name="filter",
     )(observations, transition, obs_map, measured_weighting, obs_precision, fading)
+    block = min(frames, 1024)
+    states = pl.pallas_call(
+        turn_states,
+        grid=(channels, frames // block),
+        out_shape=jax.ShapeDtypeStruct((channels, state, frames), F32),
+        in_specs=[pl.BlockSpec((1, block, state), lambda c, b: (c, b, 0))],
+        out_specs=pl.BlockSpec((1, state, block), lambda c, b: (c, 0, b)),
+        name="turn",
+    )(turned.reshape(channels, frames, state))
     return states, nis.reshape(batches)
 
 

time: 33.7 us -> 34.1 us (1.012)
  Pallas kernels: 27.7 us -> 32.7 us
  local copies, waits for them, and re-layouts: 5.17 us -> 0.52 us
    pallas_call x0 -> x1, Pallas kernels: none -> 7.88 us  [per_device(): pl.pallas_call(turn_states, grid=(channels, frames // block), out_shape=j...]
    unnamed x4 -> x3, local copies, waits for them, and re-layouts: 5.17 us -> 0.52 us
    pallas_call x1, Pallas kernels: 27.7 us -> 24.8 us  [per_device(): pl.pallas_call(functools.partial(kernel, tm, chan), out_shape=(jax.ShapeD...]
where the time goes in v1:
time: 34.1 us; the launch traced here: 33.8 us
  Pallas kernels  32.7 us (96%)
  between operations  0.65 us (2%)
  local copies, waits for them, and re-layouts  0.52 us (2%)
    pallas_call x1, Pallas kernels, per_device(): pl.pallas_call(functools.partial(kernel, tm, chan), out_shape=(jax.ShapeD...  24.8 us
    pallas_call x1, Pallas kernels, per_device(): pl.pallas_call(turn_states, grid=(channels, frames // block), out_shape=j...  7.88 us

profile of v1, /device:TPU:0, one launch (start us, length us, event | category | flops | bytes accessed | tf_op | source)
XLA Modules:
  0.0 33.8 jit_solution(9029685022681118910)
XLA Ops:
  0.6 24.8 %filter.1 = (f32[2,32,16,8,128]{4,3,2,1,0:T(8,128)}, f32[1,32]{1,0:T(1,128)}) custom-call(f32[2,64,4096]{2,1,0:T(8,128)} %y_hbm.1, f32[2,128,128]{2,1,0:T(8,128)} %trans_ref.1, f32[2,64,128]{2,1,0:T(8,128)} %map_ref.1, f32[2,64]{1,0:T(2,128)} %weight_ref.1, f32[2,64]{1,0:T(2,128)} %prec_ref.1, f32[2,4096]{1,0:T(2,128)} %fade_ref.1), custom_call_target="tpu_custom_call" | custom-call | tf_op jit(solution)/shard_map/filter/pallas_call | solution.py:283
  25.4 0.0 copy-start
  25.4 7.9 %turn.1 = f32[2,128,4096]{2,1,0:T(8,128)} custom-call(f32[2,4096,128]{2,1,0:T(8,128)} %bitcast.2), custom_call_target="tpu_custom_call" | custom-call | tf_op jit(solution)/shard_map/turn/pallas_call | solution.py:313
  33.3 0.0 copy-done
  33.3 0.5 %copy.9 = f32[32]{0:T(128)} copy(f32[32]{0:T(128)S(1)} %bitcast.3) | data formatting | bytes 256
Async XLA Ops:
  25.4 7.9 %copy-start = (f32[1,32]{1,0:T(1,128)S(1)}, f32[1,32]{1,0:T(1,128)}, u32[]{:S(2)}) copy-start(f32[1,32]{1,0:T(1,128)} %get-tuple-element.5) | copy-start | bytes 388

commit v2 on v1

v2 whole, which is shorter than its diff:
```python
import functools

import jax
import jax.numpy as jnp
from jax import lax
from jax.experimental import pallas as pl
from jax.experimental.pallas import tpu as pltpu
from jax.sharding import PartitionSpec as P

MB_FRAMES = 128
LANES = 128
GROUP = 8
PARTS = 1
SPANS = 2
CHUNK = LANES // GROUP
HIGHEST = lax.Precision.HIGHEST
F32 = jnp.float32
BF16 = jnp.bfloat16


def dot(a, b, dims=((1,), (0,)), precision=HIGHEST):
    return lax.dot_general(a, b, (dims, ((), ())), precision=precision, preferred_element_type=F32)


def halves(x):
    high = x.astype(BF16)
    low = (x - high.astype(F32)).astype(BF16)
    return high, low


def thirds(x):
    high = x.astype(BF16)
    rest = x - high.astype(F32)
    mid = rest.astype(BF16)
    return high, mid, (rest - mid.astype(F32)).astype(BF16)


def exact(a, b):
    a_high, a_mid, a_low = thirds(a)
    b_high, b_mid, b_low = thirds(b)
    top = jnp.concatenate([b_high, b_mid], axis=1)
    wide = dot(
        jnp.concatenate([a_high, a_mid], axis=1),
        jnp.concatenate([top, top], axis=0),
        precision=None,
    )
    tail = dot(
        jnp.concatenate([a_high, a_low], axis=1),
        jnp.concatenate([b_low, b_high], axis=0),
        precision=None,
    )
    half = b.shape[1]
    return wide[:, :half] + (wide[:, half:] + tail)


def rows_split(x):
    return jnp.concatenate(halves(x), axis=1)


def pack(weight):
    high, low = halves(weight)
    top = jnp.concatenate([high, low], axis=1)
    return jnp.concatenate([top, top], axis=0)


def fast(split, packed):
    both = dot(split, packed, precision=None)
    half = both.shape[1] // 2
    return both[:, :half] + both[:, half:]


def regroup(x, groups):
    place = lax.broadcasted_iota(jnp.int32, x.shape, 1)
    source = (place % groups) * (LANES // groups) + place // groups
    return jnp.take_along_axis(x, source, axis=1, mode="promise_in_bounds")


def turn_fading(fade):
    frames = fade.shape[1]
    rows = [fade[:, b : b + LANES] for b in range(0, frames, LANES)]
    filled = sum(part.shape[0] for part in rows)
    rows.append(jnp.zeros((-filled % LANES, LANES), F32))
    return jnp.transpose(regroup(jnp.concatenate(rows, axis=0), GROUP))


def fade_wide(ft_ref, step, c, channels, span):
    here = ft_ref[step * GROUP : (step + 1) * GROUP, :]
    parts = []
    for b in range(span.start, span.stop):
        lane = b * channels + c
        parts.append(jnp.broadcast_to(here[:, lane : lane + 1], (GROUP, LANES)))
    return jnp.concatenate(parts, axis=0)


def inject(values, weight):
    high, low = halves(values)
    return dot(jnp.concatenate([high, low, high], axis=1), weight, precision=None)


def shifted(x, reach, fill, row):
    return jnp.where(row >= reach, pltpu.roll(x, reach, 0), fill)


def greet(axis, size, mine):
    peers = [{axis: lax.rem(mine + d, size)} for d in range(1, size)]
    barrier = pltpu.get_barrier_semaphore()
    for target in peers:
        pl.semaphore_signal(barrier, inc=1, device_id=target, device_id_type=pl.DeviceIdType.MESH)
    return barrier, peers


def swap(src, got, send_sem, recv_sem, peers):
    sends = []
    for d, target in enumerate(peers):
        copy = pltpu.make_async_remote_copy(
            src_ref=src, dst_ref=got.at[d], send_sem=send_sem.at[d], recv_sem=recv_sem.at[d],
            device_id=target, device_id_type=pl.DeviceIdType.MESH,
        )
        copy.start()
        sends.append(copy)
    return sends


def enter_kernel(
    tm, y_hbm, trans_ref, map_ref, weight_ref, fade_ref,
    yt_hbm, ft_ref, x_ref, step_ref, pred_ref, now_ref,
    y_ref, yt_ref, end_src, end_got, in_sem, yt_sem, end_send, end_recv,
):
    channels, obs, frames = y_ref.shape
    state = trans_ref.shape[1]
    length = CHUNK
    count = frames // length
    my_tm = lax.axis_index("tm")
    barrier, peers = greet("tm", tm, my_tm)
    load = pltpu.make_async_copy(y_hbm, y_ref, in_sem)
    load.start()

    each = range(channels)
    lanes = channels * obs
    eye = lax.broadcasted_iota(jnp.int32, (obs, obs), 0) == lax.broadcasted_iota(jnp.int32, (obs, obs), 1)
    owner = lax.broadcasted_iota(jnp.int32, (1, lanes), 1) // obs

    ft_ref[...] = turn_fading(fade_ref[...])

    def fade_lanes(step):
        out = fade_wide(ft_ref, step, 0, channels, slice(0, frames // LANES))
        for c in each[1:]:
            out = jnp.where(owner == c, fade_wide(ft_ref, step, c, channels, slice(0, frames // LANES)), out)
        return out

    weighted, closed, map_trans = [], [], []
    for c in each:
        column = jnp.sum(jnp.where(eye, weight_ref[c : c + 1, :], 0.0), axis=1, keepdims=True)
        observe = map_ref[c]
        weighted.append(observe * column)
        moved = exact(observe, trans_ref[c])
        map_trans.append(jnp.transpose(moved))
        closed.append(jnp.transpose(trans_ref[c]) - exact(map_trans[c], weighted[c]))

    load.wait()
    blocks_all = frames // LANES

    def turn(first, last):
        for b in range(first, last):
            piece = y_ref[:, :, b * LANES : (b + 1) * LANES].reshape(lanes, LANES)
            yt_ref[b] = jnp.transpose(regroup(piece, GROUP)).reshape(length, GROUP, lanes)

    stacks, power = list(weighted), list(closed)
    rounds = length.bit_length() - 1
    for level in range(rounds):
        turn(level * blocks_all // rounds, (level + 1) * blocks_all // rounds)
        for c in each:
            older = fast(rows_split(stacks[c]), pack(power[c]))
            stacks[c] = jnp.concatenate([stacks[c], older], axis=0)
            power[c] = exact(power[c], power[c])

    def spread(blocks):
        rows = []
        for c in each:
            parts = [blocks[c] if d == c else jnp.zeros_like(blocks[c]) for d in each]
            rows.append(jnp.concatenate(parts, axis=1))
        return jnp.concatenate(rows, axis=0)

    def inject_weight(blocks):
        high, low = halves(spread(blocks))
        return jnp.concatenate([high, high, low], axis=0)

    def obs_at(step):
        return yt_ref[:, step].reshape(count, lanes)

    turned = pltpu.make_async_copy(yt_ref, yt_hbm, yt_sem)
    turned.start()

    ends = jnp.zeros((count, channels * state), F32)
    decay = jnp.ones((count, lanes), F32)
    packed = []
    levels = count.bit_length() - 1
    every = max(length // levels, 1)
    for step in reversed(range(length)):
        age = length - 1 - step
        blocks = [stacks[c][age * obs : (age + 1) * obs] for c in each]
        ends = ends + inject(obs_at(step) * decay, inject_weight(blocks))
        decay = decay * fade_lanes(step)
        if len(packed) < levels and age % every == 0:
            packed.append([pack(power[c]) for c in each])
            power = [exact(power[c], power[c]) for c in each]

    row = lax.broadcasted_iota(jnp.int32, (count, state), 0)
    sums = [ends[:, c * state : (c + 1) * state] for c in each]
    factors = [jnp.broadcast_to(decay[:, c * obs : c * obs + 1], (count, state)) for c in each]
    while len(packed) < levels:
        packed.append([pack(power[c]) for c in each])
        power = [exact(power[c], power[c]) for c in each]
    for level in range(levels):
        reach = 1 << level
        for c in each:
            if reach < 8:
                before = rows_split(shifted(sums[c], reach, 0.0, row))
                sums[c] = sums[c] + factors[c] * fast(before, packed[level][c])
                factors[c] = factors[c] * shifted(factors[c], reach, 1.0, row)
            else:
                rest = count - reach
                moved = factors[c][reach:] * fast(rows_split(sums[c][:rest]), packed[level][c])
                sums[c] = jnp.concatenate([sums[c][:reach], sums[c][reach:] + moved], axis=0)
                joined = factors[c][reach:] * factors[c][:rest]
                factors[c] = jnp.concatenate([factors[c][:reach], joined], axis=0)

    last = [part[c][count - 1 : count, :] for part in (sums, factors) for c in each]
    end_src[...] = jnp.concatenate(last + [jnp.zeros((8 - len(last), state), F32)], axis=0)
    pl.semaphore_wait(barrier, len(peers))
    sends = swap(end_src, end_got, end_send, end_recv, peers)

    sums = [shifted(sums[c], 1, 0.0, row) for c in each]
    factors = [shifted(factors[c], 1, 1.0, row) for c in each]
    for c in each:
        step_ref[c] = pack(closed[c])
    pred_ref[...] = jnp.concatenate(halves(spread(map_trans)), axis=1)
    now_ref[...] = inject_weight(weighted)
    section = [pack(power[c]) for c in each]

    for copy in sends:
        copy.wait()

    enter = [jnp.zeros((8, state), F32) for c in each]
    for j in range(tm - 1):
        slot = jnp.maximum(lax.rem(my_tm - j + tm, tm) - 1, 0)
        got = end_got[slot]
        for c in each:
            value = jnp.broadcast_to(got[c : c + 1, :], (8, state))
            if j > 0:
                value = value + got[channels + c : channels + c + 1, :] * fast(
                    rows_split(enter[c]), section[c]
                )
            enter[c] = jnp.where(j < my_tm, value, enter[c])

    small = lax.broadcasted_iota(jnp.int32, (8, state), 0)
    for c in each:
        carried = enter[c]
        for level, weights in enumerate(packed):
            further = fast(rows_split(carried), weights[c])
            size = 1 << level
            if size < 8:
                carried = jnp.where(small < size, carried, pltpu.roll(further, size, 0))
            else:
                carried = jnp.concatenate([carried, further], axis=0)
        x_ref[c] = sums[c] + factors[c] * carried[:count]
    turned.wait()


def step_kernel(
    yt_hbm, ft_ref, x_ref, step_ref, pred_ref, now_ref, prec_ref, states_hbm, nis_ref,
    yt_ref, xt_ref, out_ref, in_sem, out_sem,
):
    channels, count, state = x_ref.shape
    lanes = yt_ref.shape[3]
    frames = count * CHUNK
    each = range(channels)
    loads = []
    for step in range(CHUNK):
        load = pltpu.make_async_copy(yt_hbm.at[:, step], yt_ref.at[:, step], in_sem.at[step])
        load.start()
        loads.append(load)
    prec = jnp.concatenate([prec_ref[c : c + 1, :] for c in each], axis=1)
    owner = lax.broadcasted_iota(jnp.int32, (1, lanes), 1) // (lanes // channels)
    batches = nis_ref.shape[1]
    blocks = frames // LANES // PARTS
    rows = count // PARTS
    per = []
    stores = []

    def finish(b):
        for c in each:
            piece = jnp.transpose(xt_ref[c, b].reshape(LANES, state))
            out_ref[c, :, b * LANES : (b + 1) * LANES] = regroup(piece, CHUNK)

    def send(part):
        for c in each:
            span = pl.ds(part * blocks * LANES // SPANS, blocks * LANES // SPANS)
            store = pltpu.make_async_copy(
                out_ref.at[c, :, span], states_hbm.at[c, :, span], out_sem.at[c, part]
            )
            store.start()
            stores.append(store)

    waited = 0
    for part in range(PARTS):
        norms = jnp.zeros((rows, lanes), F32)
        x = [x_ref[c, part * rows : (part + 1) * rows] for c in each]
        done = 0
        for step in range(CHUNK):
            if part == 0 and step == waited:
                more = min(CHUNK, max(2, 3 * waited))
                for load in loads[waited:more]:
                    load.wait()
                waited = more
            span = slice(part * blocks, (part + 1) * blocks)
            observed = yt_ref[span, step].reshape(rows, lanes)
            wide = [fade_wide(ft_ref, step, c, channels, span) for c in each]
            mixed = wide[0]
            for c in each[1:]:
                mixed = jnp.where(owner == c, wide[c], mixed)
            added = inject(observed, now_ref[...])
            parts = [halves(x[c]) for c in each]
            rounded = jnp.concatenate([part_[0] for part_ in parts], axis=1)
            innovation = observed - mixed * fast(rounded, pred_ref[...])
            norms = norms + prec * innovation * innovation
            for c in each:
                moved = fast(jnp.concatenate(parts[c], axis=1), step_ref[c])
                x[c] = wide[c] * moved + added[:, c * state : (c + 1) * state]
                xt_ref[c, span, step] = x[c].reshape(blocks, GROUP, state)
            if part > 0:
                ready = blocks * (step + 1) // CHUNK
                for b in range(done, ready):
                    finish((part - 1) * blocks + b)
                done = ready
        if part > 0:
            for k in range(SPANS):
                send((part - 1) * SPANS + k)
        per.append(jnp.sum(norms.reshape(batches // PARTS, rows * PARTS // batches, lanes), axis=1))

    per_batch = jnp.concatenate(per, axis=0)
    nis_ref[...] = dot(jnp.ones((8, lanes), F32), per_batch, ((1,), (1,)))
    for k in range(SPANS):
        for b in range(k * blocks // SPANS, (k + 1) * blocks // SPANS):
            finish((PARTS - 1) * blocks + b)
        send((PARTS - 1) * SPANS + k)
    for store in stores:
        store.wait()


def norm_kernel(chan, divisor, mine_ref, nis_ref, got, send_sem, recv_sem):
    barrier, peers = greet("chan", chan, lax.axis_index("chan"))
    pl.semaphore_wait(barrier, len(peers))
    sends = swap(mine_ref, got, send_sem, recv_sem, peers)
    total = mine_ref[0:1, :]
    for d, copy in enumerate(sends):
        copy.wait()
        total = total + got[d, 0:1, :]
    nis_ref[...] = total / divisor


def per_device(tm, chan, observations, transition, obs_map, measured_weighting, obs_precision, fading):
    channels, obs, frames = observations.shape
    state = transition.shape[1]
    batches = frames // MB_FRAMES
    count = frames // CHUNK
    lanes = channels * obs
    vmem = pl.BlockSpec(memory_space=pltpu.VMEM)
    hbm = pl.BlockSpec(memory_space=pl.ANY)
    dma = pltpu.SemaphoreType.DMA
    shape = jax.ShapeDtypeStruct
    limit = 56 * 1024 * 1024
    turned = (frames // LANES, CHUNK, GROUP, lanes)
    handed = pl.pallas_call(
        functools.partial(enter_kernel, tm),
        out_shape=(
            shape(turned, F32),
            shape((LANES, LANES), F32),
            shape((channels, count, state), F32),
            shape((channels, 2 * state, 2 * state), BF16),
            shape((channels * state, 2 * lanes), BF16),
            shape((3 * lanes, channels * state), BF16),
        ),
        in_specs=[hbm] + [vmem] * 4,
        out_specs=(hbm,) + (vmem,) * 5,
        scratch_shapes=[
            pltpu.VMEM((channels, obs, frames), F32),
            pltpu.VMEM(turned, F32),
            pltpu.VMEM((8, state), F32),
            pltpu.VMEM((max(tm - 1, 1), 8, state), F32),
            dma(()),
            dma(()),
            dma((max(tm - 1, 1),)),
            dma((max(tm - 1, 1),)),
        ],
        compiler_params=pltpu.CompilerParams(
            collective_id=0, has_side_effects=True, vmem_limit_bytes=limit
        ),
        name="enter",
    )(observations, transition, obs_map, measured_weighting, fading)
    states, mine = pl.pallas_call(
        step_kernel,
        out_shape=(shape((channels, state, frames), F32), shape((8, batches), F32)),
        in_specs=[hbm] + [vmem] * 6,
        out_specs=(hbm, vmem),
        scratch_shapes=[
            pltpu.VMEM(turned, F32),
            pltpu.VMEM((channels, frames // LANES, CHUNK, GROUP, state), F32),
            pltpu.VMEM((channels, state, frames), F32),
            dma((CHUNK,)),
            dma((channels, PARTS * SPANS)),
        ],
        compiler_params=pltpu.CompilerParams(vmem_limit_bytes=limit),
        name="steps",
    )(*handed, obs_precision)
    nis = pl.pallas_call(
        functools.partial(norm_kernel, chan, channels * chan * MB_FRAMES * obs),
        out_shape=shape((1, batches), F32),
        in_specs=[vmem],
        out_specs=vmem,
        scratch_shapes=[
            pltpu.VMEM((max(chan - 1, 1), 8, batches), F32),
            dma((max(chan - 1, 1),)),
            dma((max(chan - 1, 1),)),
        ],
        compiler_params=pltpu.CompilerParams(collective_id=1, has_side_effects=True),
        name="norms",
    )(mine)
    return states, nis.reshape(batches)


def solution(mesh):
    in_specs = (
        P("chan", None, "tm"),
        P("chan", None, None),
        P("chan", None, None),
        P("chan", None),
        P("chan", None),
        P("chan", "tm"),
    )
    out_specs = (P("chan", None, "tm"), P("tm"))
    body = functools.partial(per_device, mesh.shape["tm"], mesh.shape["chan"])
    return jax.shard_map(body, mesh=mesh, in_specs=in_specs, out_specs=out_specs, check_vma=False)
```

time: 34.1 us -> 36.2 us (1.062)
  Pallas kernels: 32.7 us -> 34.2 us
  local copies, waits for them, and re-layouts: 0.52 us -> 1.14 us
    pallas_call x2 -> x3, Pallas kernels: 32.7 us -> 34.2 us  [the longest x1 16 us: per_device(): pl.pallas_call(functools.partial(enter_kernel, tm), out_shape=(shape(turn...]
    unnamed x3 -> x1, local copies, waits for them, and re-layouts: 0.52 us -> 1.14 us
where the time goes in v2:
time: 36.2 us; the launch traced here: 36 us
  Pallas kernels  34.2 us (94%)
  local copies, waits for them, and re-layouts  1.14 us (3%)
  between operations  0.65 us (2%)
    pallas_call x1, Pallas kernels, per_device(): pl.pallas_call(functools.partial(enter_kernel, tm), out_shape=(shape(turn...  16 us
    pallas_call x1, Pallas kernels, per_device(): pl.pallas_call(step_kernel, out_shape=(shape((channels, state, frames), F...  11 us
    pallas_call x1, Pallas kernels, per_device(): pl.pallas_call(functools.partial(norm_kernel, chan, channels * chan * MB_...  7.19 us
    unnamed x1, local copies, waits for them, and re-layouts  1.14 us

profile of v2, /device:TPU:0, one launch (start us, length us, event | category | flops | bytes accessed | tf_op | source)
XLA Modules:
  0.0 36.0 jit_solution(12784423177319343130)
XLA Ops:
  0.6 16.0 %enter.1 = (f32[32,16,8,128]{3,2,1,0:T(8,128)}, f32[128,128]{1,0:T(8,128)}, f32[2,256,128]{2,1,0:T(8,128)}, bf16[2,256,256]{2,1,0:T(8,128)(2,1)}, bf16[256,256]{1,0:T(8,128)(2,1)}, /*index=5*/bf16[384,256]{1,0:T(8,128)(2,1)}) custom-call(f32[2,64,4096]{2,1,0:T(8,128)} %y_hbm.1, f32[2,128,128]{2,1,0:T(8,128)} %trans_ref.1, f32[2,64,128]{2,1,0:T(8,128)} %map_ref.1, ...), custom_call_target="tpu_custom_call" | custom-call | tf_op jit(solution)/shard_map/enter/pallas_call | solution.py:374
  16.7 11.0 %steps.1 = (f32[2,128,4096]{2,1,0:T(8,128)}, f32[8,32]{1,0:T(8,128)}) custom-call(f32[32,16,8,128]{3,2,1,0:T(8,128)} %get-tuple-element.10.yt_hbm, f32[128,128]{1,0:T(8,128)} %get-tuple-element.11.ft_ref, f32[2,256,128]{2,1,0:T(8,128)} %get-tuple-element.12.x_ref, bf16[2,256,256]{2,1,0:T(8,128)(2,1)} %get-tuple-element.13.step_ref, ...), custom_call_target="tpu_custom_call" | custom-call | tf_op jit(solution)/shard_map/steps/pallas_call | solution.py:401
  27.6 7.2 %norms.1 = f32[1,32]{1,0:T(1,128)} custom-call(f32[8,32]{1,0:T(8,128)} %get-tuple-element.17.mine_ref), custom_call_target="tpu_custom_call" | custom-call | tf_op jit(solution)/shard_map/norms/pallas_call | solution.py:416
  34.8 1.1 %copy.9 = f32[32]{0:T(128)} copy(f32[32]{0:T(128)} %bitcast.1) | data formatting | bytes 256

commit v3 on v1

--- a/solution.py
+++ b/solution.py
@@ -26,6 +26,31 @@
     return high, low
 
 
+def thirds(x):
+    high = x.astype(BF16)
+    rest = x - high.astype(F32)
+    mid = rest.astype(BF16)
+    return high, mid, (rest - mid.astype(F32)).astype(BF16)
+
+
+def exact(a, b):
+    a_high, a_mid, a_low = thirds(a)
+    b_high, b_mid, b_low = thirds(b)
+    top = jnp.concatenate([b_high, b_mid], axis=1)
+    wide = dot(
+        jnp.concatenate([a_high, a_mid], axis=1),
+        jnp.concatenate([top, top], axis=0),
+        precision=None,
+    )
+    tail = dot(
+        jnp.concatenate([a_high, a_low], axis=1),
+        jnp.concatenate([b_low, b_high], axis=0),
+        precision=None,
+    )
+    half = b.shape[1]
+    return wide[:, :half] + (wide[:, half:] + tail)
+
+
 def rows_split(x):
     return jnp.concatenate(halves(x), axis=1)
 
@@ -54,7 +79,7 @@
 
 def kernel(
     tm, chan, y_hbm, trans_ref, map_ref, weight_ref, prec_ref, fade_ref, states_hbm, nis_ref,
-    y_ref, yt_ref, ft_ref, xt_ref, end_src, end_got, nis_src, nis_got,
+    y_ref, yt_ref, ft_ref, xt_ref, out_ref, end_src, end_got, nis_src, nis_got,
     in_sem, out_sem, end_send, end_recv, nis_send, nis_recv,
 ):
     channels, obs, frames = y_ref.shape
@@ -98,9 +123,9 @@
         column = jnp.sum(jnp.where(eye, weight_ref[c : c + 1, :], 0.0), axis=1, keepdims=True)
         observe = map_ref[c]
         weighted.append(observe * column)
-        moved = dot(observe, trans_ref[c])
+        moved = exact(observe, trans_ref[c])
         map_trans.append(jnp.transpose(moved))
-        closed.append(jnp.transpose(trans_ref[c]) - dot(moved, weighted[c], ((0,), (0,))))
+        closed.append(jnp.transpose(trans_ref[c]) - exact(map_trans[c], weighted[c]))
 
     load.wait()
     blocks_all = frames // LANES
@@ -117,7 +142,7 @@
         for c in each:
             older = fast(rows_split(stacks[c]), pack(power[c]))
             stacks[c] = jnp.concatenate([stacks[c], older], axis=0)
-            power[c] = dot(power[c], power[c])
+            power[c] = exact(power[c], power[c])
 
     def spread(blocks):
         rows = []
@@ -149,14 +174,14 @@
         decay = decay * fade_lanes(fade_at(step))
         if len(packed) < levels and age % every == 0:
             packed.append([pack(power[c]) for c in each])
-            power = [dot(power[c], power[c]) for c in each]
+            power = [exact(power[c], power[c]) for c in each]
 
     row = lax.broadcasted_iota(jnp.int32, (count, state), 0)
     sums = [ends[:, c * state : (c + 1) * state] for c in each]
     factors = [jnp.broadcast_to(decay[:, c * obs : c * obs + 1], (count, state)) for c in each]
     while len(packed) < levels:
         packed.append([pack(power[c]) for c in each])
-        power = [dot(power[c], power[c]) for c in each]
+        power = [exact(power[c], power[c]) for c in each]
     for level in range(levels):
         reach = 1 << level
         for c in each:
@@ -186,10 +211,7 @@
     sums = [shifted(sums[c], 1, 0.0, row) for c in each]
     factors = [shifted(factors[c], 1, 1.0, row) for c in each]
     step_weight = [pack(closed[c]) for c in each]
-    pred_weight = []
-    for c in each:
-        parts = [map_trans[c] if d == c else jnp.zeros_like(map_trans[c]) for d in each]
-        pred_weight.append(pack(jnp.concatenate(parts, axis=1)))
+    pred_weight = jnp.concatenate(halves(spread(map_trans)), axis=1)
     now_weight = inject_weight(weighted)
     section = [pack(power[c]) for c in each]
 
@@ -223,23 +245,21 @@
 
     prec = jnp.concatenate([prec_ref[c : c + 1, :] for c in each], axis=1)
     norms = jnp.zeros((count, lanes), F32)
-    stores = []
     for step in range(length):
         observed = obs_at(step)
         columns = fade_at(step)
         added = inject(observed, now_weight)
-        innovation = observed
-        for c in each:
-            split = rows_split(x[c])
-            wide = jnp.broadcast_to(columns[:, c : c + 1], (count, state))
-            innovation = innovation - columns[:, c : c + 1] * fast(split, pred_weight[c])
-            x[c] = wide * fast(split, step_weight[c]) + added[:, c * state : (c + 1) * state]
+        wide = [jnp.broadcast_to(columns[:, c : c + 1], (count, LANES)) for c in each]
+        mixed = wide[0]
+        for c in each[1:]:
+            mixed = jnp.where(owner == c, wide[c], mixed)
+        parts = [halves(x[c]) for c in each]
+        rounded = jnp.concatenate([part[0] for part in parts], axis=1)
+        innovation = observed - mixed * fast(rounded, pred_weight)
+        for c in each:
+            moved = fast(jnp.concatenate(parts[c], axis=1), step_weight[c])
+            x[c] = wide[c] * moved + added[:, c * state : (c + 1) * state]
             xt_ref[c, :, step] = x[c].reshape(blocks_all, GROUP, state)
-            store = pltpu.make_async_copy(
-                xt_ref.at[c, :, step], states_hbm.at[c, :, step], out_sem.at[c, step]
-            )
-            store.start()
-            stores.append(store)
         norms = norms + prec * innovation * innovation
 
     batches = nis_ref.shape[1]
@@ -255,6 +275,20 @@
         copy.start()
         sends.append(copy)
 
+    stores = []
+    block = frames // out_sem.shape[1]
+    for c in each:
+        for index in range(out_sem.shape[1]):
+            for start in range(index * block, (index + 1) * block, LANES):
+                piece = jnp.transpose(xt_ref[c, start // LANES].reshape(LANES, state))
+                out_ref[c, :, start : start + LANES] = regroup(piece, CHUNK)
+            span = pl.ds(index * block, block)
+            store = pltpu.make_async_copy(
+                out_ref.at[c, :, span], states_hbm.at[c, :, span], out_sem.at[c, index]
+            )
+            store.start()
+            stores.append(store)
+
     for copy in sends:
         copy.wait()
     total = nis_src[0:1, :]
@@ -263,12 +297,6 @@
     nis_ref[...] = total / (channels * chan * MB_FRAMES * obs)
     for store in stores:
         store.wait()
-
-
-def turn_states(x_ref, out_ref):
-    for start in range(0, x_ref.shape[1], LANES):
-        piece = jnp.transpose(x_ref[0, start : start + LANES, :])
-        out_ref[0, :, start : start + LANES] = regroup(piece, CHUNK)
 
 
 def per_device(tm, chan, observations, transition, obs_map, measured_weighting, obs_precision, fading):
@@ -280,10 +308,10 @@
     hbm = pl.BlockSpec(memory_space=pl.ANY)
     dma = pltpu.SemaphoreType.DMA
     grouped = (channels, frames // LANES, CHUNK, GROUP, state)
-    turned, nis = pl.pallas_call(
+    states, nis = pl.pallas_call(
         functools.partial(kernel, tm, chan),
         out_shape=(
-            jax.ShapeDtypeStruct(grouped, F32),
+            jax.ShapeDtypeStruct((channels, state, frames), F32),
             jax.ShapeDtypeStruct((1, batches), F32),
         ),
         in_specs=[hbm] + [vmem] * 5,
@@ -293,12 +321,13 @@
             pltpu.VMEM((frames // LANES, CHUNK, GROUP, lanes), F32),
             pltpu.VMEM((frames // LANES, CHUNK, GROUP, 8), F32),
             pltpu.VMEM(grouped, F32),
+            pltpu.VMEM((channels, state, frames), F32),
             pltpu.VMEM((8, state), F32),
             pltpu.VMEM((max(tm - 1, 1), 8, state), F32),
             pltpu.VMEM((8, batches), F32),
             pltpu.VMEM((max(chan - 1, 1), 8, batches), F32),
             dma(()),
-            dma((channels, CHUNK)),
+            dma((channels, 2)),
             dma((max(tm - 1, 1),)),
             dma((max(tm - 1, 1),)),
             dma((max(chan - 1, 1),)),
@@ -309,15 +338,6 @@
         ),
         name="filter",
     )(observations, transition, obs_map, measured_weighting, obs_precision, fading)
-    block = min(frames, 1024)
-    states = pl.pallas_call(
-        turn_states,
-        grid=(channels, frames // block),
-        out_shape=jax.ShapeDtypeStruct((channels, state, frames), F32),
-        in_specs=[pl.BlockSpec((1, block, state), lambda c, b: (c, b, 0))],
-        out_specs=pl.BlockSpec((1, state, block), lambda c, b: (c, 0, b)),
-        name="turn",
-    )(turned.reshape(channels, frames, state))
     return states, nis.reshape(batches)
 
 

time: 34.1 us -> 30.4 us (0.89)
  Pallas kernels: 32.7 us -> 24.4 us
  local copies, waits for them, and re-layouts: 0.52 us -> 5.17 us
    pallas_call x1 -> x0, Pallas kernels: 7.88 us -> none  [per_device(): pl.pallas_call(turn_states, grid=(channels, frames // block), out_shape=j...]
    unnamed x3 -> x4, local copies, waits for them, and re-layouts: 0.52 us -> 5.17 us
    pallas_call x1, Pallas kernels: 24.8 us -> 24.4 us  [per_device(): pl.pallas_call(functools.partial(kernel, tm, chan), out_shape=(jax.ShapeD...]
where the time goes in v3:
time: 30.4 us; the launch traced here: 30.2 us
  Pallas kernels  24.4 us (80%)
  local copies, waits for them, and re-layouts  5.17 us (17%)
  between operations  0.65 us (2%)
    pallas_call x1, Pallas kernels, per_device(): pl.pallas_call(functools.partial(kernel, tm, chan), out_shape=(jax.ShapeD...  24.4 us
    unnamed x4, local copies, waits for them, and re-layouts  5.17 us

profile of v3, /device:TPU:0, one launch (start us, length us, event | category | flops | bytes accessed | tf_op | source)
XLA Modules:
  0.0 30.2 jit_solution(14346640457577733705)
XLA Ops:
  0.6 24.4 %filter.1 = (f32[2,128,4096]{2,1,0:T(8,128)}, f32[1,32]{1,0:T(1,128)}) custom-call(f32[2,64,4096]{2,1,0:T(8,128)} %y_hbm.1, f32[2,128,128]{2,1,0:T(8,128)} %trans_ref.1, f32[2,64,128]{2,1,0:T(8,128)} %map_ref.1, f32[2,64]{1,0:T(2,128)} %weight_ref.1, f32[2,64]{1,0:T(2,128)} %prec_ref.1, f32[2,4096]{1,0:T(2,128)} %fade_ref.1), custom_call_target="tpu_custom_call" | custom-call | tf_op jit(solution)/shard_map/filter/pallas_call | solution.py:311
  25.0 0.0 copy-start
  25.0 4.7 %copy.10 = f32[2,128,4096]{2,1,0:T(8,128)} copy(f32[2,128,4096]{2,1,0:T(8,128)} %get-tuple-element.8) | data formatting | bytes 8388608
  29.7 0.0 copy-done
  29.7 0.5 %copy.11 = f32[32]{0:T(128)} copy(f32[32]{0:T(128)S(1)} %bitcast.1) | data formatting | bytes 256
Async XLA Ops:
  25.0 4.7 %copy-start = (f32[1,32]{1,0:T(1,128)S(1)}, f32[1,32]{1,0:T(1,128)}, u32[]{:S(2)}) copy-start(f32[1,32]{1,0:T(1,128)} %get-tuple-element.5) | copy-start | bytes 388
